TPU v7x, 32 devices: a whole 2x2x4 slice. The times are simulated.
32 devices in a mesh: inst: 4 (over x, core), dp: 4 (over z), tp: 2 (over y).
Axes of the slice: x: 2, y: 2, z: 4, core: 2. Of those that a mesh axis runs over, the one named last changes fastest.
Arguments:
- kernel_grads: bfloat16 [16, 2, 128, 4608], P(('inst', 'dp'), 'tp'), may hold values from -0.75 to 0.75
- kernel_master: float32 [2, 128, 4608], P('tp', 'dp'), may hold values from -6 to 6
- kernel_first: float32 [2, 128, 4608], P('tp', 'dp'), may hold values from -3 to 3
- kernel_second: float32 [2, 128, 4608], P('tp', 'dp'), may hold values from 0.05 to 4
- gain_grads: bfloat16 [32, 4, 4608], P(('inst', 'dp', 'tp')), may hold values from -0.29882812 to 0.29882812
- gain_master: float32 [4, 4608], replicated, may hold values from -6 to 6
- gain_first: float32 [4, 4608], replicated, may hold values from -3 to 3
- gain_second: float32 [4, 4608], replicated, may hold values from 0.05 to 4
Outputs:
- kernel_params: bfloat16 [2, 128, 4608], P('tp')
- kernel_master_new: float32 [2, 128, 4608], P('tp', 'dp')
- kernel_first_new: float32 [2, 128, 4608], P('tp', 'dp')
- kernel_second_new: float32 [2, 128, 4608], P('tp', 'dp')
- gain_params: bfloat16 [4, 4608], replicated
- gain_master_new: float32 [4, 4608], replicated
- gain_first_new: float32 [4, 4608], replicated
- gain_second_new: float32 [4, 4608], replicated
All inputs are finite; a program needn't handle non-finite values.
Results may differ from a plain program's by a relative error of at most 0.004.
Values may be sent and summed in bfloat16 or wider, within the bound.
A program may use at most 64 MiB of HBM per device.

v0:
```python
import jax
import jax.numpy as jnp
from jax import lax
from jax.sharding import PartitionSpec as P

beta_one = 0.9
beta_two = 0.95
learn_rate = 0.01
decay_rate = 0.1
epsilon = 1e-08
step_count = 100.0


def adam_update(gradient, master, first_moment, second_moment):
    first_next = beta_one * first_moment + (1.0 - beta_one) * gradient
    second_next = beta_two * second_moment + (1.0 - beta_two) * gradient * gradient
    first_hat = first_next / (1.0 - beta_one**step_count)
    second_hat = second_next / (1.0 - beta_two**step_count)
    master_next = master - learn_rate * (
        first_hat / (jnp.sqrt(second_hat) + epsilon) + decay_rate * master
    )
    return (master_next, first_next, second_next)


def local(
    kernel_grads,
    kernel_master,
    kernel_first,
    kernel_second,
    gain_grads,
    gain_master,
    gain_first,
    gain_second,
):
    local_grads = kernel_grads[0].astype(jnp.float32)
    gain_local = gain_grads[0].astype(jnp.float32)
    flat_grads = gain_local.reshape(-1)
    gain_whole = None
    partial_rows, gain_piece = (
        lax.psum_scatter(
            local_grads.astype(jnp.bfloat16), "dp", scatter_dimension=1, tiled=True
        ).astype(jnp.float32),
        lax.psum_scatter(
            flat_grads.astype(jnp.bfloat16), "dp", scatter_dimension=0, tiled=True
        ).astype(jnp.float32),
    )
    gradient, gain_piece = (
        lax.psum(partial_rows.astype(jnp.bfloat16), "inst").astype(jnp.float32),
        lax.psum(gain_piece.astype(jnp.bfloat16), "inst").astype(jnp.float32),
    )
    kernel_master_new, kernel_first_new, kernel_second_new = adam_update(
        gradient, kernel_master, kernel_first, kernel_second
    )
    kernel_params = lax.all_gather(kernel_master_new.astype(jnp.bfloat16), "dp", axis=1, tiled=True)
    gain_piece = lax.psum(gain_piece, "tp")
    gain_whole = lax.all_gather(gain_piece, "dp", axis=0, tiled=True).reshape(gain_master.shape)
    gain_master_new, gain_first_new, gain_second_new = adam_update(
        gain_whole, gain_master, gain_first, gain_second
    )
    gain_params = gain_master_new.astype(jnp.bfloat16)
    return (
        kernel_params,
        kernel_master_new,
        kernel_first_new,
        kernel_second_new,
        gain_params,
        gain_master_new,
        gain_first_new,
        gain_second_new,
    )


def solution(mesh):
    return jax.shard_map(
        local,
        mesh=mesh,
        in_specs=(
            P(("inst", "dp"), "tp", None, None),
            P("tp", "dp", None),
            P("tp", "dp", None),
            P("tp", "dp", None),
            P(("inst", "dp", "tp"), None, None),
            P(),
            P(),
            P(),
        ),
        out_specs=(
            P("tp", None, None),
            P("tp", "dp", None),
            P("tp", "dp", None),
            P("tp", "dp", None),
            P(),
            P(),
            P(),
            P(),
        ),
        check_vma=False,
    )
```

profile of v0, /device:TPU:0, one launch (start us, length us, event | category | flops | bytes accessed | tf_op | source)
XLA Modules:
  0.0 142.5 jit_solution(16182226304347898728)
XLA Ops:
  7.2 0.0 copy-start.1
  7.2 0.0 copy-start
  7.2 0.0 reduce-scatter.2.cloned.1.call-start
  7.2 0.7 reduce-scatter.2.cloned.1.call-update
  7.9 0.0 all-reduce.3.cloned.1.call-start
  8.0 34.4 %reduce-scatter.2.cloned.1.call-done = bf16[1,32,4608]{2,1,0:T(8,128)(2,1)} async-done(((bf16[1,128,4608]{2,1,0:T(8,128)(2,1)}), bf16[1,32,4608]{2,1,0:T(8,128)(2,1)}) %reduce-scatter.2.cloned.1.call-update) | async-done | bytes 294928 | tf_op jit(solution)/shard_map/reduce_scatter | solution.py:40
  42.4 0.0 all-reduce.3.cloned.1.call-update
  42.4 0.0 copy-start.5
  42.4 0.0 copy-start.6
  42.4 0.0 copy-start.2
  42.5 0.0 all-gather.3.cloned.1.call-start
  42.5 33.3 %all-reduce.3.cloned.1.call-done = bf16[1,32,4608]{2,1,0:T(8,128)(2,1)} async-done(((bf16[1,32,4608]{2,1,0:T(8,128)(2,1)}), bf16[1,32,4608]{2,1,0:T(8,128)(2,1)}) %all-reduce.3.cloned.1.call-update) | async-done | bytes 294928 | tf_op jit(solution)/shard_map/psum | solution.py:48
  75.8 0.0 copy-done
  75.8 2.7 %fusion.7 = (bf16[1,32,4608]{2,1,0:T(8,128)(2,1)}, f32[1,32,4608]{2,1,0:T(8,128)}, f32[1,32,4608]{2,1,0:T(8,128)}, f32[1,32,4608]{2,1,0:T(8,128)}) fusion(f32[1,32,4608]{2,1,0:T(8,128)S(1)} %copy-done, bf16[1,32,4608]{2,1,0:T(8,128)(2,1)} %all-reduce.3.cloned.1.call-done, f32[1,32,4608]{2,1,0:T(8,128)S(1)} %copy-done.1, f32[1,32,4608]{2,1,0:T(8,128)} %param.11), kind=kLoop, calls=%fused_computation.11 | loop fusion | flops 2506752 | bytes 4128768 | tf_op jit(solution)/shard_map/convert_element_type | solution.py:54
  78.5 0.0 all-gather.3.cloned.1.call-update
  78.6 0.6 dynamic-slice
  79.9 20.5 %all-reduce = bf16[18432]{0:T(1024)(128)(2,1)S(1)} all-reduce(bf16[18432]{0:T(1024)(128)(2,1)S(1)} %squeeze.7), channel_id=3, replica_groups=mesh['inst'=4,'dp'=4,'tp'=2] {'dp'}, use_global_device_ids=true, to_apply=%region_2.0.clone | all-reduce | flops 18432 | bytes 73728
  100.4 0.1 dynamic-slice.1
  100.5 10.9 %psum.22 = bf16[4608]{0:T(1024)(128)(2,1)S(1)} all-reduce(bf16[4608]{0:T(1024)(128)(2,1)S(1)} %dynamic-slice.1), channel_id=1, replica_groups=mesh['inst'=4,'dp'=4,'tp'=2] {'inst'}, use_global_device_ids=true, to_apply=%region_3.0 | all-reduce | flops 4608 | bytes 18432 | tf_op jit(solution)/shard_map/psum | solution.py:49
  111.4 8.2 %psum.23 = f32[4608]{0:T(1024)S(1)} all-reduce(bf16[4608]{0:T(1024)(128)(2,1)S(1)} %psum.22), channel_id=1, replica_groups=mesh['inst'=4,'dp'=4,'tp'=2] {'tp'}, use_global_device_ids=true, to_apply=%region_4.0 | all-reduce | flops 4608 | bytes 27648 | tf_op jit(solution)/shard_map/psum | solution.py:55
  119.6 13.2 %all-gather = f32[4,1,4608]{2,1,0:T(1,128)S(1)} all-gather(f32[1,1,4608]{2,1,0:T(1,128)S(1)} %reshape.22), channel_id=1, replica_groups=mesh['inst'=4,'dp'=4,'tp'=2] {'dp'}, dimensions={0}, use_global_device_ids=true | all-gather | bytes 92160 | tf_op jit(solution)/shard_map/all_gather | solution.py:56
  132.8 0.0 copy-done.4
  132.8 0.8 fusion.4
  133.6 2.4 %copy.23 = bf16[1,128,4608]{2,1,0:T(8,128)(2,1)} copy(bf16[1,128,4608]{2,1,0:T(8,128)(2,1)} %all-gather.3.cloned.1.call-done) | data formatting | bytes 2359296
  (10 shorter events, 0.0 us)
Async XLA Ops:
  7.2 68.6 %copy-start.1 = (f32[1,32,4608]{2,1,0:T(8,128)S(1)}, f32[1,32,4608]{2,1,0:T(8,128)}, u32[]{:S(2)}) copy-start(f32[1,32,4608]{2,1,0:T(8,128)} %param.10) | copy-start | bytes 1769476
  7.2 68.6 %copy-start = (f32[1,32,4608]{2,1,0:T(8,128)S(1)}, f32[1,32,4608]{2,1,0:T(8,128)}, u32[]{:S(2)}) copy-start(f32[1,32,4608]{2,1,0:T(8,128)} %param.9) | copy-start | bytes 1769476
  7.2 35.2 %reduce-scatter.2.cloned.1.call-start = ((), (), s32[]{:S(2)}) async-start(), calls=%async_computation.1 | async-start | bytes 1474560 | tf_op jit(solution)/shard_map/reduce_scatter | solution.py:40
  7.9 67.9 %all-reduce.3.cloned.1.call-start = ((), (), s32[]{:S(2)}) async-start(), calls=%async_computation.2 | async-start | bytes 589824 | tf_op jit(solution)/shard_map/psum | solution.py:48
  42.4 36.2 %copy-start.5 = (bf16[1,4,4608]{2,1,0:T(4,128)(2,1)S(1)}, bf16[1,4,4608]{2,1,0:T(4,128)(2,1)}, u32[]{:S(2)}) copy-start(bf16[1,4,4608]{2,1,0:T(4,128)(2,1)} %param.12) | copy-start | bytes 110596
  42.4 36.2 %copy-start.6 = (u32[32]{0:T(128)S(1)}, u32[32]{0:T(128)}, u32[]{:S(2)}) copy-start(u32[32]{0:T(128)} %constant.35) | copy-start | bytes 388
  42.4 90.3 %copy-start.2 = (f32[4,4608]{1,0:T(4,128)S(1)}, f32[4,4608]{1,0:T(4,128)}, u32[]{:S(2)}) copy-start(f32[4,4608]{1,0:T(4,128)} %param.13) | copy-start | bytes 221188
  42.4 90.3 %copy-start.3 = (f32[4,4608]{1,0:T(4,128)S(1)}, f32[4,4608]{1,0:T(4,128)}, u32[]{:S(2)}) copy-start(f32[4,4608]{1,0:T(4,128)} %param.14) | copy-start | bytes 221188
  42.5 90.3 %copy-start.4 = (f32[4,4608]{1,0:T(4,128)S(1)}, f32[4,4608]{1,0:T(4,128)}, u32[]{:S(2)}) copy-start(f32[4,4608]{1,0:T(4,128)} %param.15) | copy-start | bytes 221188
  42.5 91.1 %all-gather.3.cloned.1.call-start = ((), (), s32[]{:S(2)}) async-start(), calls=%async_computation.3 | async-start | bytes 1474560 | tf_op jit(solution)/shard_map/all_gather | solution.py:54
Sparse Core Ops, SparseCore 0:
  10.3 32.0 reduce-scatter.1
  44.7 31.0 all-reduce.2
  78.7 30.9 all-gather.2
where the time goes:
time: 143 us; the launch traced here: 142 us
  waiting for transfers between devices  68.4 us (48%)
  blocking collectives  52.8 us (37%)
  between operations  14.5 us (10%)
  other arithmetic  3.55 us (2%)
  local copies, waits for them, and re-layouts  3.1 us (2%)
    reduce_scatter x1, waiting for transfers between devices, local(): lax.psum_scatter(local_grads.astype(jnp.bfloat16), 'dp', scatter_dimensio...  34.4 us
    psum x1, waiting for transfers between devices, local(): lax.psum(partial_rows.astype(jnp.bfloat16), 'inst').astype(jnp.float32)  33.3 us
    unnamed x1, blocking collectives  20.5 us
    all_gather x1, blocking collectives, local(): lax.all_gather(gain_piece, 'dp', axis=0, tiled=True)  13.2 us
    psum x1, blocking collectives, local(): lax.psum(gain_piece.astype(jnp.bfloat16), 'inst').astype(jnp.float32)  10.9 us
    psum x1, blocking collectives, local(): gain_piece = lax.psum(gain_piece, 'tp')  8.21 us
    unnamed x18, local copies, waits for them, and re-layouts  3.08 us
  transfers between devices with their start and end apart: 3, of which 2 were waited for; matrix products, arithmetic and copies ran while one was open for 1% of the time, Pallas kernels for 0%

commit v1 on v0

--- a/solution.py
+++ b/solution.py
@@ -53,7 +53,9 @@
     )
     kernel_params = lax.all_gather(kernel_master_new.astype(jnp.bfloat16), "dp", axis=1, tiled=True)
     gain_piece = lax.psum(gain_piece, "tp")
-    gain_whole = lax.all_gather(gain_piece, "dp", axis=0, tiled=True).reshape(gain_master.shape)
+    gain_whole = jnp.concatenate(
+        lax.all_to_all(jnp.stack([gain_piece] * lax.axis_size("dp")), "dp", 0, 0), axis=0
+    ).reshape(gain_master.shape)
     gain_master_new, gain_first_new, gain_second_new = adam_update(
         gain_whole, gain_master, gain_first, gain_second
     )

time: 143 us -> 138 us (0.965)
  blocking collectives: 52.8 us -> 47.8 us
    all_gather x1 -> x0, blocking collectives: 13.2 us -> none  [local(): lax.all_gather(gain_piece, 'dp', axis=0, tiled=True)]
    all_to_all x0 -> x1, blocking collectives: none -> 8.13 us  [local(): lax.all_to_all(jnp.stack([gain_piece] * lax.axis_size('dp')), 'dp', 0, 0)]
    unnamed x18 -> x17, local copies, waits for them, and re-layouts: 3.08 us -> 3.06 us
where the time goes in v1:
time: 138 us; the launch traced here: 137 us
  waiting for transfers between devices  68.4 us (50%)
  blocking collectives  47.8 us (35%)
  between operations  14.5 us (11%)
  other arithmetic  3.55 us (3%)
  local copies, waits for them, and re-layouts  3.12 us (2%)
    reduce_scatter x1, waiting for transfers between devices, local(): lax.psum_scatter(local_grads.astype(jnp.bfloat16), 'dp', scatter_dimensio...  34.4 us
    psum x1, waiting for transfers between devices, local(): lax.psum(partial_rows.astype(jnp.bfloat16), 'inst').astype(jnp.float32)  33.3 us
    unnamed x1, blocking collectives  20.5 us
    psum x1, blocking collectives, local(): lax.psum(gain_piece.astype(jnp.bfloat16), 'inst').astype(jnp.float32)  10.9 us
    psum x1, blocking collectives, local(): gain_piece = lax.psum(gain_piece, 'tp')  8.21 us
    all_to_all x1, blocking collectives, local(): lax.all_to_all(jnp.stack([gain_piece] * lax.axis_size('dp')), 'dp', 0, 0)  8.13 us
    unnamed x17, local copies, waits for them, and re-layouts  3.06 us
  transfers between devices with their start and end apart: 3, of which 2 were waited for; matrix products, arithmetic and copies ran while one was open for 1% of the time, Pallas kernels for 0%

profile of v1, /device:TPU:0, one launch (start us, length us, event | category | flops | bytes accessed | tf_op | source)
XLA Modules:
  0.0 137.5 jit_solution(16669459855133718223)
XLA Ops:
  7.2 0.0 copy-start.1
  7.2 0.0 copy-start
  7.2 0.0 reduce-scatter.2.cloned.1.call-start
  7.2 0.7 reduce-scatter.2.cloned.1.call-update
  7.9 0.0 all-reduce.3.cloned.1.call-start
  8.0 34.4 %reduce-scatter.2.cloned.1.call-done = bf16[1,32,4608]{2,1,0:T(8,128)(2,1)} async-done(((bf16[1,128,4608]{2,1,0:T(8,128)(2,1)}), bf16[1,32,4608]{2,1,0:T(8,128)(2,1)}) %reduce-scatter.2.cloned.1.call-update) | async-done | bytes 294928 | tf_op jit(solution)/shard_map/reduce_scatter | solution.py:40
  42.4 0.0 all-reduce.3.cloned.1.call-update
  42.4 0.0 copy-start.5
  42.4 0.0 copy-start.6
  42.5 0.0 all-gather.2.cloned.1.call-start
  42.5 33.3 %all-reduce.3.cloned.1.call-done = bf16[1,32,4608]{2,1,0:T(8,128)(2,1)} async-done(((bf16[1,32,4608]{2,1,0:T(8,128)(2,1)}), bf16[1,32,4608]{2,1,0:T(8,128)(2,1)}) %all-reduce.3.cloned.1.call-update) | async-done | bytes 294928 | tf_op jit(solution)/shard_map/psum | solution.py:48
  75.8 0.0 copy-done
  75.8 2.7 %fusion.7 = (bf16[1,32,4608]{2,1,0:T(8,128)(2,1)}, f32[1,32,4608]{2,1,0:T(8,128)}, f32[1,32,4608]{2,1,0:T(8,128)}, f32[1,32,4608]{2,1,0:T(8,128)}) fusion(f32[1,32,4608]{2,1,0:T(8,128)S(1)} %copy-done, bf16[1,32,4608]{2,1,0:T(8,128)(2,1)} %all-reduce.3.cloned.1.call-done, f32[1,32,4608]{2,1,0:T(8,128)S(1)} %copy-done.1, f32[1,32,4608]{2,1,0:T(8,128)} %param.11), kind=kLoop, calls=%fused_computation.11 | loop fusion | flops 2506752 | bytes 4128768 | tf_op jit(solution)/shard_map/convert_element_type | solution.py:54
  78.5 0.0 all-gather.2.cloned.1.call-update
  78.6 0.6 dynamic-slice
  79.9 20.5 %all-reduce = bf16[18432]{0:T(1024)(128)(2,1)S(1)} all-reduce(bf16[18432]{0:T(1024)(128)(2,1)S(1)} %squeeze.7), channel_id=3, replica_groups=mesh['inst'=4,'dp'=4,'tp'=2] {'dp'}, use_global_device_ids=true, to_apply=%region_2.0.clone | all-reduce | flops 18432 | bytes 73728
  100.4 0.1 dynamic-slice.1
  100.5 10.9 %psum.22 = bf16[4608]{0:T(1024)(128)(2,1)S(1)} all-reduce(bf16[4608]{0:T(1024)(128)(2,1)S(1)} %dynamic-slice.1), channel_id=1, replica_groups=mesh['inst'=4,'dp'=4,'tp'=2] {'inst'}, use_global_device_ids=true, to_apply=%region_3.0 | all-reduce | flops 4608 | bytes 18432 | tf_op jit(solution)/shard_map/psum | solution.py:49
  111.4 8.2 %psum.23 = f32[4608]{0:T(1024)S(1)} all-reduce(bf16[4608]{0:T(1024)(128)(2,1)S(1)} %psum.22), channel_id=1, replica_groups=mesh['inst'=4,'dp'=4,'tp'=2] {'tp'}, use_global_device_ids=true, to_apply=%region_4.0 | all-reduce | flops 4608 | bytes 27648 | tf_op jit(solution)/shard_map/psum | solution.py:55
  119.6 8.1 %all_to_all.9 = f32[4,1,4608]{2,1,0:T(1,128)S(1)} all-to-all(f32[4,1,4608]{2,1,0:T(1,128)S(1)} %stack.2), channel_id=1, replica_groups=mesh['inst'=4,'dp'=4,'tp'=2] {'dp'}, dimensions={0} | all-to-all | bytes 147456 | tf_op jit(solution)/shard_map/all_to_all | solution.py:57
  127.8 0.0 copy-done.2
  127.8 0.0 copy-done.4
  127.8 0.8 fusion.4
  128.6 2.4 %copy.23 = bf16[1,128,4608]{2,1,0:T(8,128)(2,1)} copy(bf16[1,128,4608]{2,1,0:T(8,128)(2,1)} %all-gather.2.cloned.1.call-done) | data formatting | bytes 2359296
  (10 shorter events, 0.1 us)
Async XLA Ops:
  7.2 68.6 %copy-start.1 = (f32[1,32,4608]{2,1,0:T(8,128)S(1)}, f32[1,32,4608]{2,1,0:T(8,128)}, u32[]{:S(2)}) copy-start(f32[1,32,4608]{2,1,0:T(8,128)} %param.10) | copy-start | bytes 1769476
  7.2 68.6 %copy-start = (f32[1,32,4608]{2,1,0:T(8,128)S(1)}, f32[1,32,4608]{2,1,0:T(8,128)}, u32[]{:S(2)}) copy-start(f32[1,32,4608]{2,1,0:T(8,128)} %param.9) | copy-start | bytes 1769476
  7.2 35.2 %reduce-scatter.2.cloned.1.call-start = ((), (), s32[]{:S(2)}) async-start(), calls=%async_computation.2 | async-start | bytes 1474560 | tf_op jit(solution)/shard_map/reduce_scatter | solution.py:40
  7.9 67.9 %all-reduce.3.cloned.1.call-start = ((), (), s32[]{:S(2)}) async-start(), calls=%async_computation.3 | async-start | bytes 589824 | tf_op jit(solution)/shard_map/psum | solution.py:48
  42.4 36.2 %copy-start.5 = (bf16[1,4,4608]{2,1,0:T(4,128)(2,1)S(1)}, bf16[1,4,4608]{2,1,0:T(4,128)(2,1)}, u32[]{:S(2)}) copy-start(bf16[1,4,4608]{2,1,0:T(4,128)(2,1)} %param.12) | copy-start | bytes 110596
  42.4 36.2 %copy-start.6 = (u32[32]{0:T(128)S(1)}, u32[32]{0:T(128)}, u32[]{:S(2)}) copy-start(u32[32]{0:T(128)} %constant.35) | copy-start | bytes 388
  42.4 85.3 %copy-start.2 = (f32[4,4608]{1,0:T(4,128)S(1)}, f32[4,4608]{1,0:T(4,128)}, u32[]{:S(2)}) copy-start(f32[4,4608]{1,0:T(4,128)} %param.13) | copy-start | bytes 221188
  42.4 85.3 %copy-start.3 = (f32[4,4608]{1,0:T(4,128)S(1)}, f32[4,4608]{1,0:T(4,128)}, u32[]{:S(2)}) copy-start(f32[4,4608]{1,0:T(4,128)} %param.14) | copy-start | bytes 221188
  42.5 85.3 %copy-start.4 = (f32[4,4608]{1,0:T(4,128)S(1)}, f32[4,4608]{1,0:T(4,128)}, u32[]{:S(2)}) copy-start(f32[4,4608]{1,0:T(4,128)} %param.15) | copy-start | bytes 221188
  42.5 86.1 %all-gather.2.cloned.1.call-start = ((), (), s32[]{:S(2)}) async-start(), calls=%async_computation.4 | async-start | bytes 1474560 | tf_op jit(solution)/shard_map/all_gather | solution.py:54
Sparse Core Ops, SparseCore 0:
  10.3 32.0 reduce-scatter.1
  44.7 31.0 all-reduce.2
  78.7 30.9 all-gather.1
